TPU v7x, 16 devices: a whole 2x2x2 slice. The times are simulated.
16 devices in a mesh: data: 4 (over z, y), time: 4 (over x, core).
Axes of the slice: x: 2, y: 2, z: 2, core: 2. Of those that a mesh axis runs over, the one named last changes fastest.
Arguments:
- x_init: float32 [128, 16, 256], P('data'), parts along dimension 0
- w_in: bfloat16 [256, 1024], replicated
- w_out: bfloat16 [1024, 256], replicated
- mod_gamma: bfloat16 [32, 1024], P('time')
- mod_beta: bfloat16 [32, 1024], P('time')
- step_size: float32 [32], P('time')
Outputs:
- output: float32 [128, 16, 256], P('data'), parts along dimension 0
There are 4 independent parts. A program takes and returns all parts, laid end to end along the dimension named above; an argument that names none is the same for every part.
All inputs are finite; a program needn't handle non-finite values.
Results may differ from a plain program's by a relative error of at most 0.00135424.
Values are sent between devices in bfloat16 or wider.
A program may use at most 1 GiB of HBM per device.

v0:
```python
import jax
import jax.numpy as jnp
from jax import lax
from jax.sharding import PartitionSpec as P

SWEEPS = 4


def solution(mesh):
    groups = mesh.shape["time"]
    distances = [2 ** level for level in range(12) if 2 ** level < groups]

    def prefix_of(own_total):
        prefix = jnp.zeros_like(own_total)
        inclusive = own_total
        for distance in distances:
            send_pairs = [(source, source + distance) for source in range(groups - distance)]
            received = lax.ppermute(inclusive, "time", send_pairs)
            inclusive = inclusive + received
            prefix = prefix + received
        return prefix

    def local_run(x_init, w_in, w_out, mod_gamma, mod_beta, step_size):
        mod_scale = (1.0 + mod_gamma.astype(jnp.float32))[:, None, None, :]
        mod_shift = mod_beta.astype(jnp.float32)[:, None, None, :]
        h_steps = step_size[:, None, None, None]
        pre_act = jnp.einsum("bnc,cd->bnd", x_init.astype(jnp.bfloat16), w_in, preferred_element_type=jnp.float32)[None]
        result = x_init
        for sweep_idx in range(SWEEPS):
            hidden_act = jax.nn.gelu(pre_act * mod_scale + mod_shift, approximate=True).astype(jnp.bfloat16)
            drifts = jnp.einsum("kbnd,dc->kbnc", hidden_act, w_out, preferred_element_type=jnp.float32) * h_steps
            if sweep_idx < SWEEPS - 1:
                running = jnp.cumsum(drifts, axis=0)
                latents = x_init + prefix_of(running[-1]) + (running - drifts)
                pre_act = jnp.einsum("kbnc,cd->kbnd", latents.astype(jnp.bfloat16), w_in, preferred_element_type=jnp.float32)
            else:
                result = x_init + lax.psum(jnp.sum(drifts, axis=0), "time")
        return result

    return jax.shard_map(local_run, mesh=mesh, in_specs=(P("data", None, None), P(None, None), P(None, None), P("time", None), P("time", None), P("time")), out_specs=P("data", None, None), check_vma=False)
```

profile of v0, /device:TPU:0, one launch (start us, length us, event | category | flops | bytes accessed | tf_op | source)
XLA Modules:
  0.0 170.6 jit_solution(3845926658229016264)
XLA Ops:
  6.5 0.0 copy-start
  6.5 0.0 all-reduce.2.cloned.1.call-start
  6.5 0.8 convert_add_fusion
  7.3 0.7 convert_element_type.32
  8.0 1.6 fusion.68
  9.7 0.0 copy-done
  9.7 0.0 copy-start.7
  9.7 6.9 %fusion.32 = f32[8,32,16,256]{3,2,1,0:T(8,128)S(1)} fusion(f32[8,1024]{1,0:T(8,128)S(1)} %convert_element_type.32, f32[8,1024]{1,0:T(8,128)S(1)} %convert_add_fusion, f32[32,16,1024]{2,1,0:T(8,128)S(1)} %fusion.68, bf16[1024,256]{1,0:T(8,128)(2,1)S(1)} %copy-done), kind=kOutput, calls=%fused_computation.36 | convolution fusion | flops 2193620992 | bytes 6881280 | tf_op jit(solution)/shard_map/kbnd,dc->kbnc/dot_general | solution.py:31
  16.6 0.0 copy-done.7
  16.7 0.0 copy-start.5
  16.7 0.0 copy-start.1
  16.7 0.6 fusion.38
  17.3 1.3 copy-done.5
  18.6 0.0 copy-start.3
  18.6 0.0 copy-start.6
  18.7 2.8 %collective-permute-start = (f32[32,16,256]{2,1,0:T(8,128)S(1)}, f32[32,16,256]{2,1,0:T(8,128)S(1)}, u32[]{:S(2)}, u32[]{:S(2)}) collective-permute-start(f32[32,16,256]{2,1,0:T(8,128)S(1)} %slice_bitcast_fusion.2), channel_id=1, source_target_pairs={{0,1},{1,2},{2,3},{4,5},{5,6},{6,7},{8,9},{9,10},{10,11},{12,13},{... | collective-permute-start | bytes 1572872 | tf_op jit(solution)/shard_map/ppermute | solution.py:18
  21.5 1.5 collective-permute-done
  23.0 0.0 copy-done.3
  23.0 0.1 fusion.87
  23.1 11.7 %collective-permute-start.1 = (f32[32,16,256]{2,1,0:T(8,128)S(1)}, f32[32,16,256]{2,1,0:T(8,128)S(1)}, u32[]{:S(2)}, u32[]{:S(2)}) collective-permute-start(f32[32,16,256]{2,1,0:T(8,128)S(1)} %fusion.87), channel_id=1, source_target_pairs={{0,2},{1,3},{4,6},{5,7},{8,10},{9,11},{12,14},{13,15}} | collective-permute-start | bytes 1572872 | tf_op jit(solution)/shard_map/ppermute | solution.py:18
  34.7 8.4 %collective-permute-done.1 = f32[32,16,256]{2,1,0:T(8,128)S(1)} collective-permute-done((f32[32,16,256]{2,1,0:T(8,128)S(1)}, f32[32,16,256]{2,1,0:T(8,128)S(1)}, u32[]{:S(2)}, u32[]{:S(2)}) %collective-permute-start.1) | collective-permute-done | bytes 524320 | tf_op jit(solution)/shard_map/ppermute | solution.py:18
  43.1 0.0 copy-done.1
  43.1 0.1 add_add_fusion.2
  43.3 0.0 copy-done.6
  43.3 11.3 %fusion.42 = f32[8,32,16,256]{3,2,1,0:T(8,128)} fusion(f32[8,1024]{1,0:T(8,128)S(1)} %convert_element_type.32, f32[8,1024]{1,0:T(8,128)S(1)} %convert_add_fusion, f32[8,32,16,256]{3,2,1,0:T(8,128)} %copy-done.3, f32[8,32,16,256]{3,2,1,0:T(8,128)} %copy-done.5, f32[32,16,256]{2,1,0:T(8,128)S(1)} %add_add_fusion.2, f32[8]{0:T(128)S(1)} %copy-done.7, ...), kind=kOutput, calls=%fused_computation.49 | convolution fusion | flops 4345298944 | bytes 14221344 | tf_op jit(solution)/shard_map/kbnd,dc->kbnc/dot_general | solution.py:31
  54.6 2.8 %fusion.36 = f32[8,32,16,256]{3,2,1,0:T(8,128)S(1)} fusion(f32[8,32,16,256]{3,2,1,0:T(8,128)} %fusion.42, f32[8]{0:T(128)S(1)} %copy-done.7), kind=kOutput, calls=%fused_computation.43 | output fusion | flops 8388608 | bytes 8388640 | tf_op jit(solution)/shard_map/jit(cumsum)/reduce_window_sum | solution.py:33
  57.4 0.0 copy-start.4
  57.4 1.3 collective-permute-start.2
  58.7 1.5 collective-permute-done.2
  60.2 0.0 copy-done.4
  60.2 0.1 fusion.88
  60.3 12.1 %collective-permute-start.3 = (f32[32,16,256]{2,1,0:T(8,128)S(1)}, f32[32,16,256]{2,1,0:T(8,128)S(1)}, u32[]{:S(2)}, u32[]{:S(2)}) collective-permute-start(f32[32,16,256]{2,1,0:T(8,128)S(1)} %fusion.88), channel_id=1, source_target_pairs={{0,2},{1,3},{4,6},{5,7},{8,10},{9,11},{12,14},{13,15}} | collective-permute-start | bytes 1572872 | tf_op jit(solution)/shard_map/ppermute | solution.py:18
  72.4 8.6 %collective-permute-done.3 = f32[32,16,256]{2,1,0:T(8,128)S(1)} collective-permute-done((f32[32,16,256]{2,1,0:T(8,128)S(1)}, f32[32,16,256]{2,1,0:T(8,128)S(1)}, u32[]{:S(2)}, u32[]{:S(2)}) %collective-permute-start.3) | collective-permute-done | bytes 524320 | tf_op jit(solution)/shard_map/ppermute | solution.py:18
  81.0 0.1 add_add_fusion.1
  81.1 11.3 %fusion.41 = f32[8,32,16,256]{3,2,1,0:T(8,128)} fusion(f32[8,1024]{1,0:T(8,128)S(1)} %convert_element_type.32, f32[8,1024]{1,0:T(8,128)S(1)} %convert_add_fusion, f32[8,32,16,256]{3,2,1,0:T(8,128)} %copy-done.4, f32[8,32,16,256]{3,2,1,0:T(8,128)} %fusion.42, f32[32,16,256]{2,1,0:T(8,128)S(1)} %add_add_fusion.1, f32[8]{0:T(128)S(1)} %copy-done.7, ...), kind=kOutput, calls=%fused_computation.48 | convolution fusion | flops 4345298944 | bytes 14221344 | tf_op jit(solution)/shard_map/kbnd,dc->kbnc/dot_general | solution.py:31
  92.5 2.8 %fusion.34 = f32[8,32,16,256]{3,2,1,0:T(8,128)S(1)} fusion(f32[8,32,16,256]{3,2,1,0:T(8,128)} %fusion.41, f32[8]{0:T(128)S(1)} %copy-done.7), kind=kOutput, calls=%fused_computation.41 | output fusion | flops 8388608 | bytes 8388640 | tf_op jit(solution)/shard_map/jit(cumsum)/reduce_window_sum | solution.py:33
  95.3 0.0 copy-start.2
  95.3 1.3 collective-permute-start.4
  96.7 1.5 collective-permute-done.4
  98.1 0.0 copy-done.2
  98.1 0.1 fusion.89
  98.2 12.3 %collective-permute-start.5 = (f32[32,16,256]{2,1,0:T(8,128)S(1)}, f32[32,16,256]{2,1,0:T(8,128)S(1)}, u32[]{:S(2)}, u32[]{:S(2)}) collective-permute-start(f32[32,16,256]{2,1,0:T(8,128)S(1)} %fusion.89), channel_id=1, source_target_pairs={{0,2},{1,3},{4,6},{5,7},{8,10},{9,11},{12,14},{13,15}} | collective-permute-start | bytes 1572872 | tf_op jit(solution)/shard_map/ppermute | solution.py:18
  110.6 8.3 %collective-permute-done.5 = f32[32,16,256]{2,1,0:T(8,128)S(1)} collective-permute-done((f32[32,16,256]{2,1,0:T(8,128)S(1)}, f32[32,16,256]{2,1,0:T(8,128)S(1)}, u32[]{:S(2)}, u32[]{:S(2)}) %collective-permute-start.5) | collective-permute-done | bytes 524320 | tf_op jit(solution)/shard_map/ppermute | solution.py:18
  118.9 0.1 add_add_fusion
  119.1 11.0 %multiply_reduce_fusion = f32[32,16,256]{2,1,0:T(8,128)} fusion(f32[8]{0:T(128)S(1)} %copy-done.7, f32[8,1024]{1,0:T(8,128)S(1)} %convert_element_type.32, f32[8,1024]{1,0:T(8,128)S(1)} %convert_add_fusion, f32[8,32,16,256]{3,2,1,0:T(8,128)} %copy-done.2, f32[8,32,16,256]{3,2,1,0:T(8,128)} %fusion.41, f32[32,16,256]{2,1,0:T(8,128)S(1)} %add_add_fusion, ...), kind=kOutput, calls=%fused_computation.37 | convolution fusion | flops 4347265024 | bytes 10551328 | tf_op jit(solution)/shard_map/kbnd,dc->kbnc/dot_general | solution.py:31
  130.1 0.0 all-reduce.2.cloned.1.call-update
  130.1 31.8 %all-reduce.2.cloned.1.call-done = f32[32,16,256]{2,1,0:T(8,128)} async-done(((f32[32,16,256]{2,1,0:T(8,128)}), f32[32,16,256]{2,1,0:T(8,128)}) %all-reduce.2.cloned.1.call-update) | async-done | bytes 524304 | tf_op jit(solution)/shard_map/psum | solution.py:37
  161.9 1.9 %add.142 = f32[32,16,256]{2,1,0:T(8,128)} add(f32[32,16,256]{2,1,0:T(8,128)S(1)} %copy-done.1, f32[32,16,256]{2,1,0:T(8,128)} %all-reduce.2.cloned.1.call-done) | non-fusion elementwise | flops 131072 | bytes 1572864 | tf_op jit(solution)/shard_map/add | solution.py:37
  (3 shorter events, 0.1 us)
Async XLA Ops:
  6.5 3.1 %copy-start = (bf16[1024,256]{1,0:T(8,128)(2,1)S(1)}, bf16[1024,256]{1,0:T(8,128)(2,1)}, u32[]{:S(2)}) copy-start(bf16[1024,256]{1,0:T(8,128)(2,1)} %param.8) | copy-start | bytes 1572868
  6.5 155.4 %all-reduce.2.cloned.1.call-start = ((), (), s32[]{:S(2)}) async-start(), calls=%async_computation | async-start | bytes 1048576 | tf_op jit(solution)/shard_map/psum | solution.py:37
  9.7 7.0 %copy-start.7 = (f32[8]{0:T(128)S(1)}, f32[8]{0:T(128)}, u32[]{:S(2)}) copy-start(f32[8]{0:T(128)} %param.11) | copy-start | bytes 100
  16.7 2.0 %copy-start.5 = (f32[8,32,16,256]{3,2,1,0:T(8,128)}, f32[8,32,16,256]{3,2,1,0:T(8,128)S(1)}, u32[]{:S(2)}) copy-start(f32[8,32,16,256]{3,2,1,0:T(8,128)S(1)} %fusion.32) | copy-start | bytes 12582916
  16.7 26.4 %copy-start.1 = (f32[32,16,256]{2,1,0:T(8,128)S(1)}, f32[32,16,256]{2,1,0:T(8,128)}, u32[]{:S(2)}) copy-start(f32[32,16,256]{2,1,0:T(8,128)} %param.6) | copy-start | bytes 1572868
  18.6 4.4 %copy-start.3 = (f32[8,32,16,256]{3,2,1,0:T(8,128)}, f32[8,32,16,256]{3,2,1,0:T(8,128)S(1)}, u32[]{:S(2)}) copy-start(f32[8,32,16,256]{3,2,1,0:T(8,128)S(1)} %fusion.38) | copy-start | bytes 12582916
  18.6 24.6 %copy-start.6 = (bf16[256,1024]{1,0:T(8,128)(2,1)S(1)}, bf16[256,1024]{1,0:T(8,128)(2,1)}, u32[]{:S(2)}) copy-start(bf16[256,1024]{1,0:T(8,128)(2,1)} %param.7) | copy-start | bytes 1572868
  18.7 4.3 %collective-permute-start = (f32[32,16,256]{2,1,0:T(8,128)S(1)}, f32[32,16,256]{2,1,0:T(8,128)S(1)}, u32[]{:S(2)}, u32[]{:S(2)}) collective-permute-start(f32[32,16,256]{2,1,0:T(8,128)S(1)} %slice_bitcast_fusion.2), channel_id=1, source_target_pairs={{0,1},{1,2},{2,3},{4,5},{5,6},{6,7},{8,9},{9,10},{10,11},{12,13},{... | collective-permute-start | bytes 1572872 | tf_op jit(solution)/shard_map/ppermute | solution.py:18
  23.1 20.1 %collective-permute-start.1 = (f32[32,16,256]{2,1,0:T(8,128)S(1)}, f32[32,16,256]{2,1,0:T(8,128)S(1)}, u32[]{:S(2)}, u32[]{:S(2)}) collective-permute-start(f32[32,16,256]{2,1,0:T(8,128)S(1)} %fusion.87), channel_id=1, source_target_pairs={{0,2},{1,3},{4,6},{5,7},{8,10},{9,11},{12,14},{13,15}} | collective-permute-start | bytes 1572872 | tf_op jit(solution)/shard_map/ppermute | solution.py:18
  57.4 2.9 %copy-start.4 = (f32[8,32,16,256]{3,2,1,0:T(8,128)}, f32[8,32,16,256]{3,2,1,0:T(8,128)S(1)}, u32[]{:S(2)}) copy-start(f32[8,32,16,256]{3,2,1,0:T(8,128)S(1)} %fusion.36) | copy-start | bytes 12582916
  57.4 2.8 %collective-permute-start.2 = (f32[32,16,256]{2,1,0:T(8,128)S(1)}, f32[32,16,256]{2,1,0:T(8,128)S(1)}, u32[]{:S(2)}, u32[]{:S(2)}) collective-permute-start(f32[32,16,256]{2,1,0:T(8,128)S(1)} %slice_bitcast_fusion.1), channel_id=1, source_target_pairs={{0,1},{1,2},{2,3},{4,5},{5,6},{6,7},{8,9},{9,10},{10,11},{12,13},{... | collective-permute-start | bytes 1572872 | tf_op jit(solution)/shard_map/ppermute | solution.py:18
  60.3 20.7 %collective-permute-start.3 = (f32[32,16,256]{2,1,0:T(8,128)S(1)}, f32[32,16,256]{2,1,0:T(8,128)S(1)}, u32[]{:S(2)}, u32[]{:S(2)}) collective-permute-start(f32[32,16,256]{2,1,0:T(8,128)S(1)} %fusion.88), channel_id=1, source_target_pairs={{0,2},{1,3},{4,6},{5,7},{8,10},{9,11},{12,14},{13,15}} | collective-permute-start | bytes 1572872 | tf_op jit(solution)/shard_map/ppermute | solution.py:18
  95.3 2.9 %copy-start.2 = (f32[8,32,16,256]{3,2,1,0:T(8,128)}, f32[8,32,16,256]{3,2,1,0:T(8,128)S(1)}, u32[]{:S(2)}) copy-start(f32[8,32,16,256]{3,2,1,0:T(8,128)S(1)} %fusion.34) | copy-start | bytes 12582916
  95.3 2.8 %collective-permute-start.4 = (f32[32,16,256]{2,1,0:T(8,128)S(1)}, f32[32,16,256]{2,1,0:T(8,128)S(1)}, u32[]{:S(2)}, u32[]{:S(2)}) collective-permute-start(f32[32,16,256]{2,1,0:T(8,128)S(1)} %slice_bitcast_fusion), channel_id=1, source_target_pairs={{0,1},{1,2},{2,3},{4,5},{5,6},{6,7},{8,9},{9,10},{10,11},{12,13},{... | collective-permute-start | bytes 1572872 | tf_op jit(solution)/shard_map/ppermute | solution.py:18
  98.2 20.7 %collective-permute-start.5 = (f32[32,16,256]{2,1,0:T(8,128)S(1)}, f32[32,16,256]{2,1,0:T(8,128)S(1)}, u32[]{:S(2)}, u32[]{:S(2)}) collective-permute-start(f32[32,16,256]{2,1,0:T(8,128)S(1)} %fusion.89), channel_id=1, source_target_pairs={{0,2},{1,3},{4,6},{5,7},{8,10},{9,11},{12,14},{13,15}} | collective-permute-start | bytes 1572872 | tf_op jit(solution)/shard_map/ppermute | solution.py:18
Sparse Core Ops, SparseCore 0:
  130.2 31.6 all-reduce.1
where the time goes:
time: 171 us
  waiting for transfers between devices  61.6 us (36%)
  matrix products  42.2 us (25%)
  starting transfers between devices  41.6 us (24%)
  between operations  13.6 us (8%)
  other arithmetic  10.3 us (6%)
    ppermute x6, starting transfers between devices, prefix_of(): received = lax.ppermute(inclusive, 'time', send_pairs)  41.6 us
    dot_general x4, matrix products, local_run(): jnp.einsum('kbnd,dc->kbnc', hidden_act, w_out, preferred_element_type=jnp...  40.6 us
    psum x1, waiting for transfers between devices, local_run(): result = x_init + lax.psum(jnp.sum(drifts, axis=0), 'time')  31.8 us
    ppermute x6, waiting for transfers between devices, prefix_of(): received = lax.ppermute(inclusive, 'time', send_pairs)  29.7 us
    another operation x3, other arithmetic, local_run(): running = jnp.cumsum(drifts, axis=0)  6.18 us
  transfers between devices with their start and end apart: 7, of which 7 were waited for; matrix products, arithmetic and copies ran while one was open for 0% of the time, Pallas kernels for 0%

commit v1 on v0

v1 whole, which is shorter than its diff:
```python
import functools

import jax
import jax.numpy as jnp
from jax import lax
from jax.experimental import pallas as pl
from jax.experimental.pallas import tpu as pltpu
from jax.sharding import PartitionSpec as P

SWEEPS = 4
STEPS = 32
ROWS = 128
C = 256
H = 1024
TILE = 256
TILES = H // TILE
FIRST = [0, 32, 63, 93, 122]
U0 = 4
U1 = 5
BLOCK = 16
PIECES = 4
GELU_C = 0.7978845608028654
F32 = jnp.float32
BF16 = jnp.bfloat16
MESH = pl.DeviceIdType.MESH


def step_of(unit):
    unit = jnp.int32(unit)
    sweep = (unit >= FIRST[1]).astype(jnp.int32) + (unit >= FIRST[2]).astype(jnp.int32) + (unit >= FIRST[3]).astype(jnp.int32)
    return unit - jnp.where(sweep == 0, 0, jnp.where(sweep == 1, FIRST[1] - 1, jnp.where(sweep == 2, FIRST[2] - 2, FIRST[3] - 3)))


def kernel(h_ref, x_hbm, w_in_hbm, w_out_hbm, gamma_ref, beta_ref, y_hbm,
           w_in, w_out, gamma_raw, beta_raw, h_raw, gain, shift, hidden0, pre, act, latent, drift,
           load_sem, mod_send, mod_recv, out_sem, near_send, near_recv, far_send, far_recv, pass_send, pass_recv):
    me = lax.axis_index("time")
    group = lax.axis_index("data")
    near = me + 1 - 2 * lax.rem(me, 2)
    far = lax.rem(me + 2, 4)
    diag = lax.rem(near + 2, 4)
    peers = (near, far, diag)

    def rows_of(device):
        return pl.ds(pl.multiple_of(device * ROWS, ROWS), ROWS)

    loads = [pltpu.make_async_copy(x_hbm.at[rows_of(me)], latent.at[FIRST[1] - 1], load_sem.at[0])]
    for n in range(TILES):
        loads.append(pltpu.make_async_copy(w_in_hbm.at[:, pl.ds(n * TILE, TILE)], w_in.at[n], load_sem.at[1 + n]))
    loads.append(pltpu.make_async_copy(w_out_hbm, w_out, load_sem.at[1 + TILES]))
    for load in loads:
        load.start()

    barrier = pltpu.get_barrier_semaphore()
    for peer in peers:
        pl.semaphore_signal(barrier, inc=1, device_id=(group, peer), device_id_type=MESH)
    for k in range(8):
        h_raw[me, pl.ds(k, 1), :] = jnp.full((1, 128), h_ref[k], F32)
    gamma_raw[me] = gamma_ref[...]
    beta_raw[me] = beta_ref[...]
    pl.semaphore_wait(barrier, 3)

    sends = []
    for p, peer in enumerate(peers):
        for a, (src, dst) in enumerate(((gamma_ref, gamma_raw), (beta_ref, beta_raw), (h_raw.at[me], h_raw))):
            send = pltpu.make_async_remote_copy(
                src_ref=src, dst_ref=dst.at[me], send_sem=mod_send.at[p, a], recv_sem=mod_recv.at[me, a],
                device_id=(group, peer), device_id_type=MESH)
            send.start()
            sends.append(send)

    def dot(a, b):
        return lax.dot_general(a, b, (((1,), (0,)), ((), ())), precision=lax.Precision.DEFAULT, preferred_element_type=F32)

    for load in loads[:-1]:
        load.wait()
    x_own = latent[FIRST[1] - 1]
    for n in range(TILES):
        hidden0[:, n * TILE:(n + 1) * TILE] = dot(x_own, w_in[n])

    for peer in peers:
        for a, dst in enumerate((gamma_raw, beta_raw, h_raw)):
            pltpu.make_async_remote_copy(
                src_ref=dst.at[peer], dst_ref=dst.at[peer], send_sem=mod_send.at[0, a], recv_sem=mod_recv.at[peer, a],
                device_id=(group, peer), device_id_type=MESH).wait_recv()
    for d in range(4):
        gain[pl.ds(d * 8, 8), :] = 0.5 + 0.5 * gamma_raw[d].astype(F32)
        shift[pl.ds(d * 8, 8), :] = 0.5 * beta_raw[d].astype(F32)
    loads[-1].wait()

    def activate(src, base, n, units, shared):
        cols = slice(n * TILE, (n + 1) * TILE)
        for k in range(units):
            j = step_of(base + k)
            a = jnp.broadcast_to(gain[pl.ds(j, 1), cols], (BLOCK, TILE))
            b = jnp.broadcast_to(shift[pl.ds(j, 1), cols], (BLOCK, TILE))
            for r in range(0, ROWS, BLOCK):
                q = r if shared else k * ROWS + r
                half = src[q:q + BLOCK, cols] * a + b
                u = half * ((8 * GELU_C * 0.044715) * (half * half) + 2 * GELU_C)
                act[k * ROWS + r:k * ROWS + r + BLOCK, cols] = half * jnp.tanh(u) + half

    def project_out(units):
        drift[0:units * ROWS] = dot(act[0:units * ROWS, :], w_out[...])

    def project_in(base, units, n):
        rows = latent[pl.ds(base, units)].reshape(units * ROWS, C)
        pre[0:units * ROWS, n * TILE:(n + 1) * TILE] = dot(rows, w_in[n])

    def accumulate(base, units):
        for k in range(units):
            unit = jnp.int32(base + k)
            h = jnp.broadcast_to(h_raw[step_of(unit) // 8, pl.ds(lax.rem(step_of(unit), 8), 1), :], (ROWS, 128))
            first = (unit == FIRST[1]) | (unit == FIRST[2]) | (unit == FIRST[3])
            ahead = jnp.where(unit < FIRST[1], 32, jnp.where(unit < FIRST[2], 31, 30))
            start = jnp.where(first, unit, unit + ahead - 1)
            for c in range(0, C, 128):
                latent[unit + ahead, :, c:c + 128] = latent[start, :, c:c + 128] + drift[k * ROWS:(k + 1) * ROWS, c:c + 128] * h

    for n in range(TILES):
        activate(hidden0, 0, n, U0, True)

    def sweep0(t, carry):
        project_out(U0)
        for n in range(TILES):
            activate(hidden0, t * U0, n, U0, True)
        accumulate((t - 1) * U0, U0)
        return carry

    lax.fori_loop(1, STEPS // U0, sweep0, 0)
    project_out(U0)
    accumulate(STEPS - U0, U0)
    for n in range(TILES):
        project_in(FIRST[1], U1, n)
    for n in range(TILES):
        activate(pre, FIRST[1], n, U1, False)
        project_in(FIRST[1] + U1, U1, n)

    count = (FIRST[4] - FIRST[1]) // U1

    def later(t, carry):
        base = FIRST[1] + t * U1
        project_out(U1)
        for n in range(TILES):
            activate(pre, base + U1, n, U1, False)
            project_in(base + 2 * U1, U1, n)
        accumulate(base, U1)
        return carry

    lax.fori_loop(0, count - 2, later, 0)
    project_out(U1)
    for n in range(TILES):
        activate(pre, FIRST[4] - U1, n, U1, False)
    accumulate(FIRST[4] - 2 * U1, U1)
    project_out(U1)
    accumulate(FIRST[4] - U1, U1)

    y_own = latent.at[FIRST[4] - 1 + 30]
    piece = ROWS // PIECES

    def part(device, k):
        return pl.ds(pl.multiple_of(device * ROWS + k * piece, piece), piece)

    far_copies = []
    for k in range(PIECES):
        copy = pltpu.make_async_remote_copy(
            src_ref=y_own.at[pl.ds(k * piece, piece)], dst_ref=y_hbm.at[part(me, k)], send_sem=far_send.at[k],
            recv_sem=far_recv.at[k], device_id=(group, far), device_id_type=MESH)
        copy.start()
        far_copies.append(copy)
    near_copy = pltpu.make_async_remote_copy(
        src_ref=y_own, dst_ref=y_hbm.at[rows_of(me)], send_sem=near_send, recv_sem=near_recv,
        device_id=(group, near), device_id_type=MESH)
    near_copy.start()
    own_copy = pltpu.make_async_copy(y_own, y_hbm.at[rows_of(me)], out_sem)
    own_copy.start()
    pass_copies = []
    for k in range(PIECES):
        far_copies[k].wait_recv()
        copy = pltpu.make_async_remote_copy(
            src_ref=y_hbm.at[part(far, k)], dst_ref=y_hbm.at[part(far, k)], send_sem=pass_send.at[k],
            recv_sem=pass_recv.at[k], device_id=(group, near), device_id_type=MESH)
        copy.start()
        pass_copies.append(copy)
    near_copy.wait_recv()
    for copy in pass_copies:
        copy.wait_recv()
    own_copy.wait()
    near_copy.wait_send()
    for copy in far_copies + pass_copies + sends:
        copy.wait_send()


def solution(mesh):
    vmem = pltpu.VMEM
    units = max(U0, U1)

    def local_run(x_init, w_in, w_out, mod_gamma, mod_beta, step_size):
        hbm = pl.BlockSpec(memory_space=pl.ANY)
        out = pl.pallas_call(
            kernel,
            out_shape=jax.ShapeDtypeStruct((4 * ROWS, C), F32),
            in_specs=[pl.BlockSpec(memory_space=pltpu.SMEM), hbm, hbm, hbm, pl.BlockSpec(memory_space=vmem), pl.BlockSpec(memory_space=vmem)],
            out_specs=hbm,
            scratch_shapes=[
                vmem((TILES, C, TILE), BF16), vmem((H, C), BF16),
                vmem((4, 8, H), BF16), vmem((4, 8, H), BF16), vmem((4, 8, 128), F32),
                vmem((STEPS, H), F32), vmem((STEPS, H), F32),
                vmem((ROWS, H), F32), vmem((units * ROWS, H), F32), vmem((units * ROWS, H), F32),
                vmem((FIRST[4] + 32, ROWS, C), F32), vmem((units * ROWS, C), F32),
                pltpu.SemaphoreType.DMA((2 + TILES,)),
                pltpu.SemaphoreType.DMA((3, 3)), pltpu.SemaphoreType.DMA((4, 3)),
                pltpu.SemaphoreType.DMA, pltpu.SemaphoreType.DMA, pltpu.SemaphoreType.DMA,
                pltpu.SemaphoreType.DMA((PIECES,)), pltpu.SemaphoreType.DMA((PIECES,)),
                pltpu.SemaphoreType.DMA((PIECES,)), pltpu.SemaphoreType.DMA((PIECES,)),
            ],
            compiler_params=pltpu.CompilerParams(collective_id=0, has_side_effects=True, vmem_limit_bytes=60 * 2 ** 20),
            name="picard",
        )(step_size, x_init.reshape(4 * ROWS, C), w_in, w_out, mod_gamma, mod_beta)
        return out.reshape(x_init.shape)

    return jax.shard_map(local_run, mesh=mesh, in_specs=(P("data", None, None), P(None, None), P(None, None), P("time", None), P("time", None), P("time")), out_specs=P("data", None, None), check_vma=False)
```

time: 171 us -> 38.5 us (0.23)
  waiting for transfers between devices: 61.6 us -> 0 us
  matrix products: 42.2 us -> 0 us
  starting transfers between devices: 41.6 us -> 0 us
  Pallas kernels: 0 us -> 36.4 us
  between operations: 13.6 us -> 0.01 us
  other arithmetic: 10.3 us -> 0 us
    dot_general x5 -> x0, matrix products: 42.2 us -> none  [the longest x4 40.6 us: local_run(): jnp.einsum('kbnd,dc->kbnc', hidden_act, w_out, preferred_element_type=jnp...]
    ppermute x6 -> x0, starting transfers between devices: 41.6 us -> none  [prefix_of(): received = lax.ppermute(inclusive, 'time', send_pairs)]
    pallas_call x0 -> x1, Pallas kernels: none -> 36.4 us  [local_run(): pl.pallas_call(kernel, out_shape=jax.ShapeDtypeStruct((4 * ROWS, C), F32)...]
    psum x1 -> x0, waiting for transfers between devices: 31.8 us -> none  [local_run(): result = x_init + lax.psum(jnp.sum(drifts, axis=0), 'time')]
    ppermute x6 -> x0, waiting for transfers between devices: 29.7 us -> none  [prefix_of(): received = lax.ppermute(inclusive, 'time', send_pairs)]
    another operation x3 -> x0, other arithmetic: 6.18 us -> none  [local_run(): running = jnp.cumsum(drifts, axis=0)]
    add x8 -> x0, other arithmetic: 3.37 us -> none  [the longest x1 1.91 us: local_run(): result = x_init + lax.psum(jnp.sum(drifts, axis=0), 'time')]
  transfers between devices with their start and end apart: 7 -> 0, of which waited for: 7 -> 0; matrix products, arithmetic and copies ran while one was open for 0% -> 0% of each run, Pallas kernels for 0% -> 0%
where the time goes in v1:
time: 38.5 us; the launch traced here: 38.3 us
  Pallas kernels  36.4 us (95%)
  local copies, waits for them, and re-layouts  1.87 us (5%)
    pallas_call x1, Pallas kernels, local_run(): pl.pallas_call(kernel, out_shape=jax.ShapeDtypeStruct((4 * ROWS, C), F32)...  36.4 us
    unnamed x1, local copies, waits for them, and re-layouts  1.87 us

profile of v1, /device:TPU:0, one launch (start us, length us, event | category | flops | bytes accessed | tf_op | source)
XLA Modules:
  0.0 38.3 jit_solution(11217704736810147660)
XLA Ops:
  0.0 36.4 %picard.1 = f32[512,256]{1,0:T(8,128)} custom-call(f32[8]{0:T(128)} %h_ref.1, f32[512,256]{1,0:T(8,128)} %bitcast.3, bf16[256,1024]{1,0:T(8,128)(2,1)} %w_in_hbm.1, bf16[1024,256]{1,0:T(8,128)(2,1)} %w_out_hbm.1, bf16[8,1024]{1,0:T(8,128)(2,1)} %gamma_ref.1, bf16[8,1024]{1,0:T(8,128)(2,1)} %beta_ref.1), custom_call_target="tpu_custom_call" | custom-call | tf_op jit(solution)/shard_map/picard/pallas_call | solution.py:200
  36.4 1.9 %copy.8 = f32[32,16,256]{2,1,0:T(8,128)} copy(f32[32,16,256]{2,1,0:T(8,128)} %bitcast.2) | data formatting | bytes 1048576

commit v2 on v0

v2 whole, which is shorter than its diff:
```python
import jax
import jax.numpy as jnp
from jax import lax
from jax.experimental import pallas as pl
from jax.experimental.pallas import tpu as pltpu
from jax.sharding import PartitionSpec as P

STEPS = 32
OWN = 8
ROWS = 128
C = 256
H = 1024
TILE = 256
TILES = H // TILE
FIRST = [0, 32, 63, 93, 122]
UNITS = 6
TAIL = 18
SECTION = 32
SECTIONS = ROWS // SECTION
CHUNKS = (FIRST[4] - TAIL - FIRST[1]) // UNITS
BATCH = UNITS * ROWS
TAIL_BATCH = TAIL * SECTION
STRIP = 16
GELU_C = 0.7978845608028654
F32 = jnp.float32
BF16 = jnp.bfloat16
MESH = pl.DeviceIdType.MESH


def span(first, count):
    return slice(first, first + count) if isinstance(first, int) else pl.ds(first, count)


def sweep_values(unit, values):
    if isinstance(unit, int):
        return values[0] if unit < FIRST[2] else values[1] if unit < FIRST[3] else values[2]
    return jnp.where(unit < FIRST[2], values[0], jnp.where(unit < FIRST[3], values[1], values[2]))


def step_of(unit):
    return unit - sweep_values(unit, (FIRST[1] - 1, FIRST[2] - 2, FIRST[3] - 3))


def kernel(h_hbm, x_hbm, w_in_hbm, w_out_hbm, gamma_hbm, beta_hbm, y,
           w_in, w_out, gamma_raw, beta_raw, h_own, h_rows, gain, shift, hidden0, pre, act, latent, drift, drift0,
           load_sem, mod_send, mod_recv, near_send, near_recv, far_send, far_recv, pass_send, pass_recv):
    me = lax.axis_index("time")
    group = lax.axis_index("data")
    core = lax.rem(me, 2)
    near = me + 1 - 2 * core
    far = lax.rem(me + 2, 4)
    diag = lax.rem(near + 2, 4)
    peers = (near, far, diag)

    def rows_of(device, first=0, count=ROWS):
        return pl.ds(pl.multiple_of(device * ROWS + first, 8), count)

    def steps_of(device):
        return pl.ds(pl.multiple_of(device * OWN, OWN), OWN)

    loads = [
        pltpu.make_async_copy(gamma_hbm, gamma_raw.at[me], load_sem.at[0]),
        pltpu.make_async_copy(beta_hbm, beta_raw.at[me], load_sem.at[1]),
        pltpu.make_async_copy(h_hbm, h_own, load_sem.at[2]),
        pltpu.make_async_copy(x_hbm.at[rows_of(me)], latent.at[FIRST[1] - 1], load_sem.at[3]),
    ]
    for n in range(TILES):
        loads.append(pltpu.make_async_copy(w_in_hbm.at[:, pl.ds(n * TILE, TILE)], w_in.at[n], load_sem.at[4 + n]))
    loads.append(pltpu.make_async_copy(w_out_hbm, w_out, load_sem.at[4 + TILES]))
    for load in loads:
        load.start()

    barrier = pltpu.get_barrier_semaphore()
    for peer in peers:
        pl.semaphore_signal(barrier, inc=1, device_id=(group, peer), device_id_type=MESH)
    for load in loads[:3]:
        load.wait()
    for k in range(OWN):
        h_rows[pl.ds(me * OWN + k, 1), :] = jnp.broadcast_to(h_own[:, k:k + 1], (1, 128))
    pl.semaphore_wait(barrier, 3)

    def mod_copy(p, peer, source):
        refs = (gamma_raw.at[source], beta_raw.at[source], h_rows.at[steps_of(source)])
        return [
            pltpu.make_async_remote_copy(
                src_ref=ref, dst_ref=ref, send_sem=mod_send.at[p, a], recv_sem=mod_recv.at[source, a],
                device_id=(group, peer), device_id_type=MESH)
            for a, ref in enumerate(refs)
        ]

    sends = []
    for p, peer in enumerate(peers):
        sends += mod_copy(p, peer, me)
    for send in sends:
        send.start()

    def dot(a, b):
        return lax.dot_general(a, b, (((1,), (0,)), ((), ())), precision=lax.Precision.DEFAULT, preferred_element_type=F32)

    def modulation(device):
        gain[steps_of(device), :] = 0.5 + 0.5 * gamma_raw[device].astype(F32)
        shift[steps_of(device), :] = 0.5 * beta_raw[device].astype(F32)

    def gelu(pre_act, a, b):
        half = pre_act * a + b
        u = half * ((8 * GELU_C * 0.044715) * (half * half) + 2 * GELU_C)
        return half * jnp.tanh(u) + half

    def activate(source, n, count, rows, mod, shared=False):
        cols = slice(n * TILE, (n + 1) * TILE)
        for k in range(count):
            a, b = mod(k, cols)
            for r in range(0, rows, STRIP):
                q = r if shared else k * rows + r
                act[k * rows + r:k * rows + r + STRIP, cols] = gelu(source[q:q + STRIP, cols], a, b)

    def mod_rows(steps):
        def rows(k, cols):
            row = span(steps[k], 1)
            return jnp.broadcast_to(gain[row, cols], (STRIP, TILE)), jnp.broadcast_to(shift[row, cols], (STRIP, TILE))
        return rows

    for load in loads[3:-1]:
        load.wait()
    modulation(me)
    x_own = latent[FIRST[1] - 1]
    for n in range(TILES):
        hidden0[:, n * TILE:(n + 1) * TILE] = dot(x_own, w_in[n])

    def steps0(device):
        return mod_rows([device * OWN + k for k in range(OWN)])

    def project0(device):
        half = OWN * ROWS // 2
        for i in range(2):
            rows = pl.ds(pl.multiple_of(device * (OWN * ROWS) + i * half, half), half)
            drift0[rows] = dot(act[i * half:(i + 1) * half, :], w_out[...])

    def chain0(first, last):
        for r in range(0, ROWS, 64):
            for c in range(0, C, 128):
                total = latent[FIRST[1] - 1 + first, r:r + 64, c:c + 128]
                for j in range(first, last):
                    h = jnp.broadcast_to(h_rows[j:j + 1, :], (64, 128))
                    total = total + drift0[j * ROWS + r:j * ROWS + r + 64, c:c + 128] * h
                    latent[FIRST[1] + j, r:r + 64, c:c + 128] = total

    other = 2 - 2 * (me // 2)

    def ordered(k):
        if isinstance(k, int):
            return (me, near, other, other + 1)[k]
        return jnp.where(k == 0, me, jnp.where(k == 1, near, other + k - 2))

    for n in range(TILES):
        activate(hidden0, n, OWN, ROWS, steps0(me), True)
    loads[-1].wait()

    def loop0(k, carry):
        for copy in mod_copy(0, near, ordered(k)):
            copy.wait_recv()
        modulation(ordered(k))
        project0(ordered(k - 1))
        for n in range(TILES):
            activate(hidden0, n, OWN, ROWS, steps0(ordered(k)), True)
        return carry

    lax.fori_loop(1, 4, loop0, 0)

    def chunk(t):
        return FIRST[1] + t * UNITS

    def unit_mods(base):
        return mod_rows([step_of(base + k) for k in range(UNITS)])

    def project_in(base, n):
        rows = latent[span(base, UNITS)].reshape(BATCH, C)
        pre[:, n * TILE:(n + 1) * TILE] = dot(rows, w_in[n])

    def project_out(count, parts=1):
        rows = count // parts
        return [dot(act[i * rows:(i + 1) * rows, :], w_out[...]) for i in range(parts)]

    def keep(drifts):
        first = 0
        for part in drifts:
            drift[first:first + part.shape[0]] = part
            first += part.shape[0]

    def accumulate(base, idle=None):
        for k in range(UNITS):
            unit = base + k
            if idle is not None:
                unit = jnp.where(idle, FIRST[4] - 1, unit)
            h = jnp.broadcast_to(h_rows[span(step_of(unit), 1), :], (ROWS, 128))
            ahead = sweep_values(unit, (31, 30, 30))
            if isinstance(unit, int):
                start = unit if unit in FIRST else unit + ahead - 1
            else:
                start = jnp.where((unit == FIRST[1]) | (unit == FIRST[2]) | (unit == FIRST[3]), unit, unit + ahead - 1)
            for c in range(0, C, 128):
                latent[unit + ahead, :, c:c + 128] = latent[start, :, c:c + 128] + drift[k * ROWS:(k + 1) * ROWS, c:c + 128] * h

    parity = []

    def step(body):
        parity.append(0)
        pl.when(me < 4 if len(parity) % 2 else me >= 0)(body)

    chain0(0, OWN)

    @step
    def _():
        for n in range(TILES):
            project_in(chunk(0), n)
        project0(ordered(3))
        for n in range(TILES):
            activate(pre, n, UNITS, ROWS, unit_mods(chunk(0)))

    @step
    def _():
        chain0(OWN, 2 * OWN)
        for n in range(TILES - 1):
            project_in(chunk(1), n)
        chain0(2 * OWN, STEPS)

    def loop(t, carry):
        base = chunk(t)
        project_in(base + UNITS, TILES - 1)
        drifts = project_out(BATCH)
        for n in range(TILES):
            activate(pre, n, UNITS, ROWS, unit_mods(base + UNITS))
            if n < TILES - 1:
                project_in(base + 2 * UNITS, n)
        accumulate(base - UNITS, t == 0)
        keep(drifts)
        return carry

    lax.fori_loop(0, CHUNKS - 2, loop, 0)

    tail = mod_rows(list(range(STEPS - TAIL, STEPS)))

    def section_in(q, n):
        rows = latent[FIRST[4] - TAIL:FIRST[4], q * SECTION:(q + 1) * SECTION].reshape(TAIL_BATCH, C)
        pre[0:TAIL_BATCH, n * TILE:(n + 1) * TILE] = dot(rows, w_in[n])

    def finish(q):
        for c in range(0, C, 128):
            total = latent[FIRST[4] - TAIL - 1 + 30, q * SECTION:(q + 1) * SECTION, c:c + 128]
            for k in range(TAIL):
                h = jnp.broadcast_to(h_rows[STEPS - TAIL + k:STEPS - TAIL + k + 1, :], (SECTION, 128))
                total = total + drift[k * SECTION:(k + 1) * SECTION, c:c + 128] * h
            y[rows_of(me, q * SECTION, SECTION), c:c + 128] = total

    def section_copy(q, source, target, send, recv):
        ref = y.at[rows_of(source, q * SECTION, SECTION)]
        return pltpu.make_async_remote_copy(
            src_ref=ref, dst_ref=ref, send_sem=send.at[q], recv_sem=recv.at[q], device_id=(group, target), device_id_type=MESH)

    def section_copies(q):
        return [section_copy(q, me, far, far_send, far_recv), section_copy(q, me, near, near_send, near_recv)]

    def send_section(q):
        for copy in section_copies(q):
            copy.start()

    def into(t, n):
        if t < CHUNKS:
            project_in(chunk(t), n)
        elif t < CHUNKS + SECTIONS:
            section_in(t - CHUNKS, n)

    def through(t, n):
        if t < CHUNKS:
            activate(pre, n, UNITS, ROWS, unit_mods(chunk(t)))
        elif t < CHUNKS + SECTIONS:
            activate(pre, n, TAIL, SECTION, tail)

    def tail_step(t):
        def body():
            into(t + 1, TILES - 1)
            if t <= CHUNKS:
                accumulate(chunk(t - 1))
            drifts = project_out(BATCH if t < CHUNKS else TAIL_BATCH)
            for n in range(TILES):
                through(t + 1, n)
                if n < TILES - 1:
                    into(t + 2, n)
            keep(drifts)
        return body

    for t in range(CHUNKS - 2, CHUNKS + SECTIONS - 1):
        if t > CHUNKS:
            step(lambda: finish(t - 1 - CHUNKS))
            send_section(t - 1 - CHUNKS)
        step(tail_step(t))
    step(lambda: finish(SECTIONS - 2))
    send_section(SECTIONS - 2)

    @step
    def _():
        keep(project_out(TAIL_BATCH, 2))
        finish(SECTIONS - 1)

    send_section(SECTIONS - 1)

    own_copies = [section_copies(q) for q in range(SECTIONS)]
    pass_copies = [section_copy(q, far, near, pass_send, pass_recv) for q in range(SECTIONS)]
    for (far_copy, _), pass_copy in zip(own_copies, pass_copies):
        far_copy.wait_recv()
        pass_copy.start()
    for (_, near_copy), pass_copy in zip(own_copies, pass_copies):
        near_copy.wait_recv()
        pass_copy.wait_recv()
    for copy in sends + [copy for copies in own_copies for copy in copies] + pass_copies:
        copy.wait_send()


def solution(mesh):
    vmem = pltpu.VMEM
    dma = pltpu.SemaphoreType.DMA
    sections = dma((SECTIONS,))
    def local_run(x_init, w_in, w_out, mod_gamma, mod_beta, step_size):
        hbm = pl.BlockSpec(memory_space=pl.ANY)
        out = pl.pallas_call(
            kernel,
            out_shape=vmem((4 * ROWS, C), F32),
            in_specs=[hbm] * 6,
            out_specs=pl.BlockSpec(memory_space=vmem),
            scratch_shapes=[
                vmem((TILES, C, TILE), BF16), vmem((H, C), BF16),
                vmem((4, OWN, H), BF16), vmem((4, OWN, H), BF16), vmem((1, OWN), F32), vmem((STEPS, 128), F32),
                vmem((STEPS, H), F32), vmem((STEPS, H), F32),
                vmem((ROWS, H), F32), vmem((BATCH, H), F32), vmem((OWN * ROWS, H), F32),
                vmem((FIRST[4] + 32, ROWS, C), F32), vmem((BATCH, C), F32), vmem((STEPS * ROWS, C), F32),
                dma((5 + TILES,)), dma((3, 3)), dma((4, 3)),
                sections, sections, sections, sections, sections, sections,
            ],
            compiler_params=pltpu.CompilerParams(collective_id=0, has_side_effects=True, vmem_limit_bytes=60 * 2 ** 20),
            name="picard",
        )(step_size.reshape(1, OWN), x_init.reshape(4 * ROWS, C), w_in, w_out, mod_gamma, mod_beta)
        return out.reshape(x_init.shape)

    return jax.shard_map(local_run, mesh=mesh, in_specs=(P("data", None, None), P(None, None), P(None, None), P("time", None), P("time", None), P("time")), out_specs=P("data", None, None), check_vma=False)
```

time: 171 us -> 33.7 us (0.20)
  waiting for transfers between devices: 61.6 us -> 0 us
  matrix products: 42.2 us -> 0 us
  starting transfers between devices: 41.6 us -> 0 us
  Pallas kernels: 0 us -> 32.7 us
  between operations: 13.6 us -> 0.01 us
  other arithmetic: 10.3 us -> 0 us
    dot_general x5 -> x0, matrix products: 42.2 us -> none  [the longest x4 40.6 us: local_run(): jnp.einsum('kbnd,dc->kbnc', hidden_act, w_out, preferred_element_type=jnp...]
    ppermute x6 -> x0, starting transfers between devices: 41.6 us -> none  [prefix_of(): received = lax.ppermute(inclusive, 'time', send_pairs)]
    pallas_call x0 -> x1, Pallas kernels: none -> 32.7 us  [local_run(): pl.pallas_call(kernel, out_shape=vmem((4 * ROWS, C), F32), in_specs=[hbm]...]
    psum x1 -> x0, waiting for transfers between devices: 31.8 us -> none  [local_run(): result = x_init + lax.psum(jnp.sum(drifts, axis=0), 'time')]
    ppermute x6 -> x0, waiting for transfers between devices: 29.7 us -> none  [prefix_of(): received = lax.ppermute(inclusive, 'time', send_pairs)]
    another operation x3 -> x0, other arithmetic: 6.18 us -> none  [local_run(): running = jnp.cumsum(drifts, axis=0)]
    add x8 -> x0, other arithmetic: 3.37 us -> none  [the longest x1 1.91 us: local_run(): result = x_init + lax.psum(jnp.sum(drifts, axis=0), 'time')]
  transfers between devices with their start and end apart: 7 -> 0, of which waited for: 7 -> 0; matrix products, arithmetic and copies ran while one was open for 0% -> 0% of each run, Pallas kernels for 0% -> 0%
where the time goes in v2:
time: 33.7 us; the launch traced here: 33.5 us
  Pallas kernels  32.7 us (97%)
  local copies, waits for them, and re-layouts  0.8 us (2%)
    pallas_call x1, Pallas kernels, local_run(): pl.pallas_call(kernel, out_shape=vmem((4 * ROWS, C), F32), in_specs=[hbm]...  32.7 us
    unnamed x1, local copies, waits for them, and re-layouts  0.8 us

profile of v2, /device:TPU:0, one launch (start us, length us, event | category | flops | bytes accessed | tf_op | source)
XLA Modules:
  0.0 33.5 jit_solution(9111943042243612715)
XLA Ops:
  0.0 32.7 %picard.1 = f32[512,256]{1,0:T(8,128)S(1)} custom-call(f32[1,8]{1,0:T(1,128)} %bitcast.5, f32[512,256]{1,0:T(8,128)} %bitcast.4, bf16[256,1024]{1,0:T(8,128)(2,1)} %w_in_hbm.1, bf16[1024,256]{1,0:T(8,128)(2,1)} %w_out_hbm.1, bf16[8,1024]{1,0:T(8,128)(2,1)} %gamma_hbm.1, bf16[8,1024]{1,0:T(8,128)(2,1)} %beta_hbm.1), custom_call_target="tpu_custom_call" | custom-call | tf_op jit(solution)/shard_map/picard/pallas_call | solution.py:325
  32.7 0.8 %copy.8 = f32[32,16,256]{2,1,0:T(8,128)} copy(f32[32,16,256]{2,1,0:T(8,128)S(1)} %bitcast.3) | data formatting | bytes 1048576

commit v3 on v2

--- a/solution.py
+++ b/solution.py
@@ -73,10 +73,8 @@
     barrier = pltpu.get_barrier_semaphore()
     for peer in peers:
         pl.semaphore_signal(barrier, inc=1, device_id=(group, peer), device_id_type=MESH)
-    for load in loads[:3]:
+    for load in loads[:2]:
         load.wait()
-    for k in range(OWN):
-        h_rows[pl.ds(me * OWN + k, 1), :] = jnp.broadcast_to(h_own[:, k:k + 1], (1, 128))
     pl.semaphore_wait(barrier, 3)
 
     def mod_copy(p, peer, source):
@@ -91,8 +89,9 @@
     sends = []
     for p, peer in enumerate(peers):
         sends += mod_copy(p, peer, me)
-    for send in sends:
-        send.start()
+    for a, send in enumerate(sends):
+        if a % 3 < 2:
+            send.start()
 
     def dot(a, b):
         return lax.dot_general(a, b, (((1,), (0,)), ((), ())), precision=lax.Precision.DEFAULT, preferred_element_type=F32)
@@ -120,9 +119,11 @@
             return jnp.broadcast_to(gain[row, cols], (STRIP, TILE)), jnp.broadcast_to(shift[row, cols], (STRIP, TILE))
         return rows
 
-    for load in loads[3:-1]:
+    for load in loads[2:-1]:
         load.wait()
     modulation(me)
+    for k in range(OWN):
+        h_rows[pl.ds(me * OWN + k, 1), :] = jnp.broadcast_to(h_own[:, k:k + 1], (1, 128))
     x_own = latent[FIRST[1] - 1]
     for n in range(TILES):
         hidden0[:, n * TILE:(n + 1) * TILE] = dot(x_own, w_in[n])
@@ -154,10 +155,12 @@
 
     for n in range(TILES):
         activate(hidden0, n, OWN, ROWS, steps0(me), True)
+    for send in sends[2::3]:
+        send.start()
     loads[-1].wait()
 
     def loop0(k, carry):
-        for copy in mod_copy(0, near, ordered(k)):
+        for copy in mod_copy(0, near, ordered(k))[:2]:
             copy.wait_recv()
         modulation(ordered(k))
         project0(ordered(k - 1))
@@ -166,6 +169,8 @@
         return carry
 
     lax.fori_loop(1, 4, loop0, 0)
+    for k in range(1, 4):
+        mod_copy(0, near, ordered(k))[2].wait_recv()
 
     def chunk(t):
         return FIRST[1] + t * UNITS
@@ -201,28 +206,30 @@
             for c in range(0, C, 128):
                 latent[unit + ahead, :, c:c + 128] = latent[start, :, c:c + 128] + drift[k * ROWS:(k + 1) * ROWS, c:c + 128] * h
 
-    parity = []
-
-    def step(body):
-        parity.append(0)
-        pl.when(me < 4 if len(parity) % 2 else me >= 0)(body)
+    def steps(*bodies):
+        def turn(i, carry):
+            for k, body in enumerate(bodies):
+                pl.when(i == k)(body)
+            return carry
+
+        lax.fori_loop(0, len(bodies), turn, 0)
 
     chain0(0, OWN)
 
-    @step
-    def _():
+    def first_chunk():
         for n in range(TILES):
             project_in(chunk(0), n)
         project0(ordered(3))
         for n in range(TILES):
             activate(pre, n, UNITS, ROWS, unit_mods(chunk(0)))
 
-    @step
-    def _():
+    def second_chunk():
         chain0(OWN, 2 * OWN)
         for n in range(TILES - 1):
             project_in(chunk(1), n)
         chain0(2 * OWN, STEPS)
+
+    steps(first_chunk, second_chunk)
 
     def loop(t, carry):
         base = chunk(t)
@@ -258,7 +265,10 @@
             src_ref=ref, dst_ref=ref, send_sem=send.at[q], recv_sem=recv.at[q], device_id=(group, target), device_id_type=MESH)
 
     def section_copies(q):
-        return [section_copy(q, me, far, far_send, far_recv), section_copy(q, me, near, near_send, near_recv)]
+        copies = [section_copy(q, me, far, far_send, far_recv), section_copy(q, me, near, near_send, near_recv)]
+        if q == SECTIONS - 1:
+            copies.append(section_copy(q, me, diag, pass_send, pass_recv))
+        return copies
 
     def send_section(q):
         for copy in section_copies(q):
@@ -278,6 +288,13 @@
 
     def tail_step(t):
         def body():
+            if t > CHUNKS:
+                finish(t - 1 - CHUNKS)
+                send_section(t - 1 - CHUNKS)
+            if t + 1 == CHUNKS + SECTIONS:
+                keep(project_out(TAIL_BATCH, 2))
+                finish(SECTIONS - 1)
+                return
             into(t + 1, TILES - 1)
             if t <= CHUNKS:
                 accumulate(chunk(t - 1))
@@ -289,29 +306,20 @@
             keep(drifts)
         return body
 
-    for t in range(CHUNKS - 2, CHUNKS + SECTIONS - 1):
-        if t > CHUNKS:
-            step(lambda: finish(t - 1 - CHUNKS))
-            send_section(t - 1 - CHUNKS)
-        step(tail_step(t))
-    step(lambda: finish(SECTIONS - 2))
-    send_section(SECTIONS - 2)
-
-    @step
-    def _():
-        keep(project_out(TAIL_BATCH, 2))
-        finish(SECTIONS - 1)
-
+    steps(tail_step(CHUNKS - 2), tail_step(CHUNKS - 1))
+    steps(tail_step(CHUNKS), tail_step(CHUNKS + 1))
+    steps(tail_step(CHUNKS + 2), tail_step(CHUNKS + 3))
     send_section(SECTIONS - 1)
 
     own_copies = [section_copies(q) for q in range(SECTIONS)]
-    pass_copies = [section_copy(q, far, near, pass_send, pass_recv) for q in range(SECTIONS)]
-    for (far_copy, _), pass_copy in zip(own_copies, pass_copies):
-        far_copy.wait_recv()
-        pass_copy.start()
-    for (_, near_copy), pass_copy in zip(own_copies, pass_copies):
-        near_copy.wait_recv()
-        pass_copy.wait_recv()
+    pass_copies = [section_copy(q, far, near, pass_send, pass_recv) for q in range(SECTIONS - 1)]
+    for q, copies in enumerate(own_copies):
+        copies[0].wait_recv()
+        if q < SECTIONS - 1:
+            pass_copies[q].start()
+    for q, copies in enumerate(own_copies):
+        copies[1].wait_recv()
+        (pass_copies[q] if q < SECTIONS - 1 else copies[2]).wait_recv()
     for copy in sends + [copy for copies in own_copies for copy in copies] + pass_copies:
         copy.wait_send()
 

time: 33.7 us -> 33.3 us (0.988)
  Pallas kernels: 32.7 us -> 32.3 us
    pallas_call x1, Pallas kernels: 32.7 us -> 32.3 us  [local_run(): pl.pallas_call(kernel, out_shape=vmem((4 * ROWS, C), F32), in_specs=[hbm]...]
where the time goes in v3:
time: 33.3 us; the launch traced here: 33.1 us
  Pallas kernels  32.3 us (97%)
  local copies, waits for them, and re-layouts  0.8 us (2%)
    pallas_call x1, Pallas kernels, local_run(): pl.pallas_call(kernel, out_shape=vmem((4 * ROWS, C), F32), in_specs=[hbm]...  32.3 us
    unnamed x1, local copies, waits for them, and re-layouts  0.8 us

profile of v3, /device:TPU:0, one launch (start us, length us, event | category | flops | bytes accessed | tf_op | source)
XLA Modules:
  0.0 33.1 jit_solution(6241258259819494216)
XLA Ops:
  0.0 32.3 %picard.1 = f32[512,256]{1,0:T(8,128)S(1)} custom-call(f32[1,8]{1,0:T(1,128)} %bitcast.5, f32[512,256]{1,0:T(8,128)} %bitcast.4, bf16[256,1024]{1,0:T(8,128)(2,1)} %w_in_hbm.1, bf16[1024,256]{1,0:T(8,128)(2,1)} %w_out_hbm.1, bf16[8,1024]{1,0:T(8,128)(2,1)} %gamma_hbm.1, bf16[8,1024]{1,0:T(8,128)(2,1)} %beta_hbm.1), custom_call_target="tpu_custom_call" | custom-call | tf_op jit(solution)/shard_map/picard/pallas_call | solution.py:333
  32.3 0.8 %copy.8 = f32[32,16,256]{2,1,0:T(8,128)} copy(f32[32,16,256]{2,1,0:T(8,128)S(1)} %bitcast.3) | data formatting | bytes 1048576

commit v4 on v3

--- a/solution.py
+++ b/solution.py
@@ -20,6 +20,7 @@
 CHUNKS = (FIRST[4] - TAIL - FIRST[1]) // UNITS
 BATCH = UNITS * ROWS
 TAIL_BATCH = TAIL * SECTION
+EARLY = (FIRST[3] - 2 - FIRST[1]) // UNITS >= CHUNKS - 2
 STRIP = 16
 GELU_C = 0.7978845608028654
 F32 = jnp.float32
@@ -192,11 +193,9 @@
             drift[first:first + part.shape[0]] = part
             first += part.shape[0]
 
-    def accumulate(base, idle=None):
+    def accumulate(base):
         for k in range(UNITS):
             unit = base + k
-            if idle is not None:
-                unit = jnp.where(idle, FIRST[4] - 1, unit)
             h = jnp.broadcast_to(h_rows[span(step_of(unit), 1), :], (ROWS, 128))
             ahead = sweep_values(unit, (31, 30, 30))
             if isinstance(unit, int):
@@ -239,8 +238,8 @@
             activate(pre, n, UNITS, ROWS, unit_mods(base + UNITS))
             if n < TILES - 1:
                 project_in(base + 2 * UNITS, n)
-        accumulate(base - UNITS, t == 0)
         keep(drifts)
+        accumulate(base)
         return carry
 
     lax.fori_loop(0, CHUNKS - 2, loop, 0)
@@ -288,27 +287,42 @@
 
     def tail_step(t):
         def body():
-            if t > CHUNKS:
-                finish(t - 1 - CHUNKS)
-                send_section(t - 1 - CHUNKS)
-            if t + 1 == CHUNKS + SECTIONS:
-                keep(project_out(TAIL_BATCH, 2))
-                finish(SECTIONS - 1)
-                return
             into(t + 1, TILES - 1)
-            if t <= CHUNKS:
-                accumulate(chunk(t - 1))
-            drifts = project_out(BATCH if t < CHUNKS else TAIL_BATCH)
+            drifts = project_out(BATCH if t < CHUNKS else TAIL_BATCH, 2 if EARLY and t == CHUNKS - 2 else 1)
+            if EARLY and t == CHUNKS - 2:
+                keep(drifts)
+                accumulate(chunk(t))
             for n in range(TILES):
                 through(t + 1, n)
                 if n < TILES - 1:
                     into(t + 2, n)
-            keep(drifts)
+            if not (EARLY and t == CHUNKS - 2):
+                keep(drifts)
+                if t < CHUNKS:
+                    accumulate(chunk(t))
+            if t >= CHUNKS:
+                finish(t - CHUNKS)
+                send_section(t - CHUNKS)
         return body
+
+    def before_last():
+        into(CHUNKS + SECTIONS - 1, TILES - 1)
+        drifts = project_out(TAIL_BATCH, 2)
+        for n in range(2):
+            through(CHUNKS + SECTIONS - 1, n)
+        keep(drifts)
+        finish(SECTIONS - 2)
+        send_section(SECTIONS - 2)
+
+    def last():
+        for n in range(2, TILES):
+            through(CHUNKS + SECTIONS - 1, n)
+        keep(project_out(TAIL_BATCH, 2))
+        finish(SECTIONS - 1)
 
     steps(tail_step(CHUNKS - 2), tail_step(CHUNKS - 1))
     steps(tail_step(CHUNKS), tail_step(CHUNKS + 1))
-    steps(tail_step(CHUNKS + 2), tail_step(CHUNKS + 3))
+    steps(before_last, last)
     send_section(SECTIONS - 1)
 
     own_copies = [section_copies(q) for q in range(SECTIONS)]

time: 33.3 us -> 32.9 us (0.988)
  Pallas kernels: 32.3 us -> 31.9 us
    pallas_call x1, Pallas kernels: 32.3 us -> 31.9 us  [local_run(): pl.pallas_call(kernel, out_shape=vmem((4 * ROWS, C), F32), in_specs=[hbm]...]
where the time goes in v4:
time: 32.9 us; the launch traced here: 32.7 us
  Pallas kernels  31.9 us (97%)
  local copies, waits for them, and re-layouts  0.8 us (2%)
    pallas_call x1, Pallas kernels, local_run(): pl.pallas_call(kernel, out_shape=vmem((4 * ROWS, C), F32), in_specs=[hbm]...  31.9 us
    unnamed x1, local copies, waits for them, and re-layouts  0.8 us

profile of v4, /device:TPU:0, one launch (start us, length us, event | category | flops | bytes accessed | tf_op | source)
XLA Modules:
  0.0 32.7 jit_solution(1445524821933477814)
XLA Ops:
  0.0 31.9 %picard.1 = f32[512,256]{1,0:T(8,128)S(1)} custom-call(f32[1,8]{1,0:T(1,128)} %bitcast.5, f32[512,256]{1,0:T(8,128)} %bitcast.4, bf16[256,1024]{1,0:T(8,128)(2,1)} %w_in_hbm.1, bf16[1024,256]{1,0:T(8,128)(2,1)} %w_out_hbm.1, bf16[8,1024]{1,0:T(8,128)(2,1)} %gamma_hbm.1, bf16[8,1024]{1,0:T(8,128)(2,1)} %beta_hbm.1), custom_call_target="tpu_custom_call" | custom-call | tf_op jit(solution)/shard_map/picard/pallas_call | solution.py:347
  31.9 0.8 %copy.8 = f32[32,16,256]{2,1,0:T(8,128)} copy(f32[32,16,256]{2,1,0:T(8,128)S(1)} %bitcast.3) | data formatting | bytes 1048576

commit v5 on v4

--- a/solution.py
+++ b/solution.py
@@ -193,17 +193,17 @@
             drift[first:first + part.shape[0]] = part
             first += part.shape[0]
 
-    def accumulate(base):
+    def accumulate(base, drifts=None):
         for k in range(UNITS):
             unit = base + k
-            h = jnp.broadcast_to(h_rows[span(step_of(unit), 1), :], (ROWS, 128))
+            h = h_rows[span(step_of(unit), 1), :]
+            h = jnp.broadcast_to(jnp.concatenate([h, h], axis=1), (ROWS, C))
             ahead = sweep_values(unit, (31, 30, 30))
             if isinstance(unit, int):
                 start = unit if unit in FIRST else unit + ahead - 1
             else:
                 start = jnp.where((unit == FIRST[1]) | (unit == FIRST[2]) | (unit == FIRST[3]), unit, unit + ahead - 1)
-            for c in range(0, C, 128):
-                latent[unit + ahead, :, c:c + 128] = latent[start, :, c:c + 128] + drift[k * ROWS:(k + 1) * ROWS, c:c + 128] * h
+            latent[unit + ahead] = latent[start] + (drift if drifts is None else drifts)[k * ROWS:(k + 1) * ROWS] * h
 
     def steps(*bodies):
         def turn(i, carry):
@@ -238,8 +238,7 @@
             activate(pre, n, UNITS, ROWS, unit_mods(base + UNITS))
             if n < TILES - 1:
                 project_in(base + 2 * UNITS, n)
-        keep(drifts)
-        accumulate(base)
+        accumulate(base, drifts[0])
         return carry
 
     lax.fori_loop(0, CHUNKS - 2, loop, 0)

time: 32.9 us -> 32.8 us (level)
  no operation moved by 1% of the time
where the time goes in v5:
time: 32.8 us; the launch traced here: 32.6 us
  Pallas kernels  31.8 us (97%)
  local copies, waits for them, and re-layouts  0.8 us (2%)
    pallas_call x1, Pallas kernels, local_run(): pl.pallas_call(kernel, out_shape=vmem((4 * ROWS, C), F32), in_specs=[hbm]...  31.8 us
    unnamed x1, local copies, waits for them, and re-layouts  0.8 us

profile of v5, /device:TPU:0, one launch (start us, length us, event | category | flops | bytes accessed | tf_op | source)
XLA Modules:
  0.0 32.6 jit_solution(11958644039480790179)
XLA Ops:
  0.0 31.8 %picard.1 = f32[512,256]{1,0:T(8,128)S(1)} custom-call(f32[1,8]{1,0:T(1,128)} %bitcast.5, f32[512,256]{1,0:T(8,128)} %bitcast.4, bf16[256,1024]{1,0:T(8,128)(2,1)} %w_in_hbm.1, bf16[1024,256]{1,0:T(8,128)(2,1)} %w_out_hbm.1, bf16[8,1024]{1,0:T(8,128)(2,1)} %gamma_hbm.1, bf16[8,1024]{1,0:T(8,128)(2,1)} %beta_hbm.1), custom_call_target="tpu_custom_call" | custom-call | tf_op jit(solution)/shard_map/picard/pallas_call | solution.py:346
  31.8 0.8 %copy.8 = f32[32,16,256]{2,1,0:T(8,128)} copy(f32[32,16,256]{2,1,0:T(8,128)S(1)} %bitcast.3) | data formatting | bytes 1048576

commit v6 on v5

--- a/solution.py
+++ b/solution.py
@@ -307,14 +307,14 @@
     def before_last():
         into(CHUNKS + SECTIONS - 1, TILES - 1)
         drifts = project_out(TAIL_BATCH, 2)
-        for n in range(2):
+        for n in range(3):
             through(CHUNKS + SECTIONS - 1, n)
         keep(drifts)
         finish(SECTIONS - 2)
         send_section(SECTIONS - 2)
 
     def last():
-        for n in range(2, TILES):
+        for n in range(3, TILES):
             through(CHUNKS + SECTIONS - 1, n)
         keep(project_out(TAIL_BATCH, 2))
         finish(SECTIONS - 1)

time: 32.8 us -> 32.8 us (level)
  no operation moved by 1% of the time
where the time goes in v6:
time: 32.8 us; the launch traced here: 32.6 us
  Pallas kernels  31.8 us (97%)
  local copies, waits for them, and re-layouts  0.8 us (2%)
    pallas_call x1, Pallas kernels, local_run(): pl.pallas_call(kernel, out_shape=vmem((4 * ROWS, C), F32), in_specs=[hbm]...  31.8 us
    unnamed x1, local copies, waits for them, and re-layouts  0.8 us

profile of v6, /device:TPU:0, one launch (start us, length us, event | category | flops | bytes accessed | tf_op | source)
XLA Modules:
  0.0 32.6 jit_solution(17099338825600417924)
XLA Ops:
  0.0 31.8 %picard.1 = f32[512,256]{1,0:T(8,128)S(1)} custom-call(f32[1,8]{1,0:T(1,128)} %bitcast.5, f32[512,256]{1,0:T(8,128)} %bitcast.4, bf16[256,1024]{1,0:T(8,128)(2,1)} %w_in_hbm.1, bf16[1024,256]{1,0:T(8,128)(2,1)} %w_out_hbm.1, bf16[8,1024]{1,0:T(8,128)(2,1)} %gamma_hbm.1, bf16[8,1024]{1,0:T(8,128)(2,1)} %beta_hbm.1), custom_call_target="tpu_custom_call" | custom-call | tf_op jit(solution)/shard_map/picard/pallas_call | solution.py:346
  31.8 0.8 %copy.8 = f32[32,16,256]{2,1,0:T(8,128)} copy(f32[32,16,256]{2,1,0:T(8,128)S(1)} %bitcast.3) | data formatting | bytes 1048576
